TPU v7x, 32 devices: a whole 2x2x4 slice. The times are simulated.
32 devices in a mesh: sector: 16 (over z, y, x), block: 2 (over core).
Axes of the slice: x: 2, y: 2, z: 4, core: 2. Of those that a mesh axis runs over, the one named last changes fastest.
Arguments:
- adjoint_prev: float32 [5, 16, 128, 128], P(None, 'block', 'sector'), may hold values from -6 to 6
- adjoint_source: float32 [5, 16, 128, 128], P(None, 'block', 'sector'), may hold values from -6 to 6
- face_matrices: bfloat16 [3, 5, 5, 16, 128, 128], P(None, None, None, 'block', 'sector'), may hold values from -2.5 to 2.5
- inverse_blocks: bfloat16 [5, 5, 16, 128, 128], P(None, None, 'block', 'sector')
- sector_offset: int32 [1], replicated, may hold values from 1 to 15
- donor_cells: int32 [128], P('sector'), may hold values from 0 to 7
- donor_weights: float32 [128], P('sector'), may hold values from 0.1 to 0.9
Outputs:
- adjoint: float32 [5, 16, 128, 128], P(None, 'block', 'sector')
- last_update: float32 [5, 16, 128, 128], P(None, 'block', 'sector')
All inputs are finite; a program needn't handle non-finite values.
Results may differ from a plain program's by a relative error of at most 0.0003.
Values sent between devices are 32-bit elements; how exact they have to be, the bound alone decides.
No kernel may reach another device: no remote copies, remote signals or barrier semaphores. Data moves between devices by JAX's collectives and lax.ppermute only.
A program may use at most 64 MiB of HBM per device.

v0:
```python
import jax
import jax.numpy as jnp
from jax import lax
from jax.sharding import PartitionSpec as P

ITERS = 4


def passed_along(value, axis, steps):
    count = lax.axis_size(axis)
    pairs = [(source, (source + steps) % count) for source in range(count)]
    return lax.ppermute(value, axis, pairs)


def padded(cells, sides, width, closed):
    for axis, dim in sides:
        count = lax.axis_size(axis)
        ends = count if closed else count - 1
        head = lax.slice_in_dim(cells, 0, width, axis=dim)
        tail = lax.slice_in_dim(cells, cells.shape[dim] - width, cells.shape[dim], axis=dim)
        cells = jnp.concatenate(
            [
                lax.ppermute(tail, axis, [(i, (i + 1) % count) for i in range(ends)]),
                cells,
                lax.ppermute(head, axis, [((i + 1) % count, i) for i in range(ends)]),
            ],
            axis=dim,
        )
    return cells


def shards(
    adjoint_prev,
    adjoint_source,
    face_matrices,
    inverse_blocks,
    sector_offset,
    donor_cells,
    donor_weights,
):
    sectors = lax.axis_size("sector")
    blocks = lax.axis_size("block")
    block_index = lax.axis_index("block")
    cells_around = adjoint_prev.shape[2]
    offset_value = sector_offset[0]
    columns = jnp.arange(cells_around + 1, dtype=jnp.int32)
    first_hit = (columns[None, :] == donor_cells[:, None]).astype(jnp.float32)
    second_hit = (columns[None, :] == donor_cells[:, None] + 1).astype(jnp.float32)
    blend_table = donor_weights[:, None] * first_hit + (1.0 - donor_weights[:, None]) * second_hit
    adjoint = adjoint_prev
    last_update = jnp.zeros_like(adjoint_prev)
    for sweep_number in range(ITERS):
        beside_all = padded(adjoint, (("sector", 2),), 1, True)
        along = padded(adjoint, (("block", 1),), 1, False)
        sweep_lower_rim = along[:, 0]
        upper_rim = along[:, -1]
        around_minus = beside_all[:, :, :-2]
        around_plus = beside_all[:, :, 2:]
        following = passed_along(sweep_lower_rim[:, :1], "sector", -1)
        extended = jnp.concatenate([sweep_lower_rim, following], axis=1)
        moved_rows = extended
        for bit_number in range((sectors - 1).bit_length()):
            hopped = passed_along(moved_rows, "sector", 1 << bit_number)
            moved_rows = jnp.where(offset_value >> bit_number & 1 == 1, hopped, moved_rows)
        facing = jnp.einsum("jk,nkr->njr", blend_table, moved_rows, precision=lax.Precision.HIGHEST)
        sweep_lower_rim = jnp.where(block_index == blocks // 2, facing, sweep_lower_rim)
        axial_minus = jnp.concatenate([sweep_lower_rim[:, None], adjoint[:, :-1]], axis=1)
        axial_plus = jnp.concatenate([adjoint[:, 1:], upper_rim[:, None]], axis=1)
        radial_pad = jnp.pad(adjoint, ((0, 0), (0, 0), (0, 0), (1, 1)))
        mixed = (
            0.6 * axial_minus + 0.4 * axial_plus,
            0.6 * around_minus + 0.4 * around_plus,
            0.6 * radial_pad[:, :, :, :-2] + 0.4 * radial_pad[:, :, :, 2:],
        )
        coupled = jnp.zeros_like(adjoint)
        for direction in range(3):
            for comp in range(5):
                coupled = (
                    coupled
                    + face_matrices[direction, comp].astype(jnp.float32)
                    * mixed[direction][comp][None]
                )
        total = adjoint_source + coupled
        result = jnp.zeros_like(adjoint)
        for comp in range(5):
            result = result + inverse_blocks[:, comp].astype(jnp.float32) * total[comp][None]
        last_update = result - adjoint
        adjoint = result
    return (adjoint, last_update)


def solution(mesh):
    return jax.shard_map(
        shards,
        mesh=mesh,
        in_specs=(
            P(None, "block", "sector", None),
            P(None, "block", "sector", None),
            P(None, None, None, "block", "sector", None),
            P(None, None, "block", "sector", None),
            P(),
            P("sector"),
            P("sector"),
        ),
        out_specs=(P(None, "block", "sector", None), P(None, "block", "sector", None)),
        check_vma=False,
    )
```

profile of v0, /device:TPU:0, one launch (start us, length us, event | category | flops | bytes accessed | tf_op | source)
XLA Modules:
  0.0 140.0 jit_solution(11164335714284014732)
XLA Ops:
  1.4 2.4 %collective-permute-start = (f32[5,1,8,128]{3,2,0,1:T(8,128)S(1)}, f32[5,1,8,128]{3,2,0,1:T(8,128)S(1)}, u32[]{:S(2)}, u32[]{:S(2)}) collective-permute-start(f32[5,1,8,128]{3,2,0,1:T(8,128)S(1)} %get-tuple-element.108), channel_id=1, source_target_pairs={{0,1},{2,3},{4,5},{6,7},{8,9},{10,11},{12,13},{14,15},{16,17},{18,... | collective-permute-start | bytes 61448 | tf_op jit(solution)/shard_map/ppermute | solution.py:23
  3.8 1.3 collective-permute-start.6
  6.2 2.4 %collective-permute-start.7 = (f32[5,8,1,128]{3,2,0,1:T(1,128)S(1)}, f32[5,8,1,128]{3,2,0,1:T(1,128)S(1)}, u32[]{:S(2)}, u32[]{:S(2)}) collective-permute-start(f32[5,8,1,128]{3,2,0,1:T(1,128)S(1)} %get-tuple-element.116), channel_id=1, source_target_pairs={{0,2},{2,4},{4,6},{6,8},{8,10},{10,12},{12,14},{14,16},{16,18},{18... | collective-permute-start | bytes 61448 | tf_op jit(solution)/shard_map/ppermute | solution.py:23
  8.5 4.1 %collective-permute-start.8 = (f32[5,8,1,128]{3,2,0,1:T(1,128)S(1)}, f32[5,8,1,128]{3,2,0,1:T(1,128)S(1)}, u32[]{:S(2)}, u32[]{:S(2)}) collective-permute-start(f32[5,8,1,128]{3,2,0,1:T(1,128)S(1)} %get-tuple-element.117), channel_id=1, source_target_pairs={{2,0},{4,2},{6,4},{8,6},{10,8},{12,10},{14,12},{16,14},{18,16},{20... | collective-permute-start | bytes 61448 | tf_op jit(solution)/shard_map/ppermute | solution.py:25
  13.6 2.0 %collective-permute-start.1 = (f32[5,1,128]{2,1,0:T(1,128)S(1)}, f32[5,1,128]{2,1,0:T(1,128)S(1)}, u32[]{:S(2)}, u32[]{:S(2)}) collective-permute-start(f32[5,1,128]{2,1,0:T(1,128)S(1)} %slice.645), channel_id=1, source_target_pairs={{0,30},{2,0},{4,2},{6,4},{8,6},{10,8},{12,10},{14,12},{16,14},{18,... | collective-permute-start | bytes 7688 | tf_op jit(solution)/shard_map/ppermute | solution.py:12
  17.9 6.9 %collective-permute-done.2 = f32[5,9,128]{2,1,0:T(8,128)S(1)} collective-permute-done((f32[5,9,128]{2,1,0:T(8,128)S(1)}, f32[5,9,128]{2,1,0:T(8,128)S(1)}, u32[]{:S(2)}, u32[]{:S(2)}) %collective-permute-start.2) | collective-permute-done | bytes 23072 | tf_op jit(solution)/shard_map/ppermute | solution.py:12
  25.0 6.7 %collective-permute-done.3 = f32[5,9,128]{2,1,0:T(8,128)S(1)} collective-permute-done((f32[5,9,128]{2,1,0:T(8,128)S(1)}, f32[5,9,128]{2,1,0:T(8,128)S(1)}, u32[]{:S(2)}, u32[]{:S(2)}) %collective-permute-start.3) | collective-permute-done | bytes 23072 | tf_op jit(solution)/shard_map/ppermute | solution.py:12
  31.9 5.6 %collective-permute-done.4 = f32[5,9,128]{2,1,0:T(8,128)S(1)} collective-permute-done((f32[5,9,128]{2,1,0:T(8,128)S(1)}, f32[5,9,128]{2,1,0:T(8,128)S(1)}, u32[]{:S(2)}, u32[]{:S(2)}) %collective-permute-start.4) | collective-permute-done | bytes 23072 | tf_op jit(solution)/shard_map/ppermute | solution.py:12
  37.6 4.9 %collective-permute-done.5 = f32[5,9,128]{2,1,0:T(8,128)S(1)} collective-permute-done((f32[5,9,128]{2,1,0:T(8,128)S(1)}, f32[5,9,128]{2,1,0:T(8,128)S(1)}, u32[]{:S(2)}, u32[]{:S(2)}) %collective-permute-start.5) | collective-permute-done | bytes 23072 | tf_op jit(solution)/shard_map/ppermute | solution.py:12
  43.2 1.3 collective-permute-start.9
  45.3 3.6 %collective-permute-done.10 = f32[5,1,128]{2,1,0:T(1,128)S(1)} collective-permute-done((f32[5,1,128]{2,1,0:T(1,128)S(1)}, f32[5,1,128]{2,1,0:T(1,128)S(1)}, u32[]{:S(2)}, u32[]{:S(2)}) %collective-permute-start.10) | collective-permute-done | bytes 2592 | tf_op jit(solution)/shard_map/ppermute | solution.py:12
  48.9 1.3 collective-permute-start.15
  50.3 5.7 %collective-permute-start.17 = (f32[5,8,1,128]{3,2,0,1:T(1,128)S(1)}, f32[5,8,1,128]{3,2,0,1:T(1,128)S(1)}, u32[]{:S(2)}, u32[]{:S(2)}) collective-permute-start(f32[5,8,1,128]{3,2,0,1:T(1,128)S(1)} %get-tuple-element.89), channel_id=1, source_target_pairs={{2,0},{4,2},{6,4},{8,6},{10,8},{12,10},{14,12},{16,14},{18,16},{20... | collective-permute-start | bytes 61448 | tf_op jit(solution)/shard_map/ppermute | solution.py:25
  56.5 1.1 collective-permute-done.16
  57.8 5.4 %collective-permute-done.12 = f32[5,9,128]{2,1,0:T(8,128)S(1)} collective-permute-done((f32[5,9,128]{2,1,0:T(8,128)S(1)}, f32[5,9,128]{2,1,0:T(8,128)S(1)}, u32[]{:S(2)}, u32[]{:S(2)}) %collective-permute-start.12) | collective-permute-done | bytes 23072 | tf_op jit(solution)/shard_map/ppermute | solution.py:12
  63.3 6.1 %collective-permute-done.13 = f32[5,9,128]{2,1,0:T(8,128)S(1)} collective-permute-done((f32[5,9,128]{2,1,0:T(8,128)S(1)}, f32[5,9,128]{2,1,0:T(8,128)S(1)}, u32[]{:S(2)}, u32[]{:S(2)}) %collective-permute-start.13) | collective-permute-done | bytes 23072 | tf_op jit(solution)/shard_map/ppermute | solution.py:12
  69.4 4.9 %collective-permute-done.14 = f32[5,9,128]{2,1,0:T(8,128)S(1)} collective-permute-done((f32[5,9,128]{2,1,0:T(8,128)S(1)}, f32[5,9,128]{2,1,0:T(8,128)S(1)}, u32[]{:S(2)}, u32[]{:S(2)}) %collective-permute-start.14) | collective-permute-done | bytes 23072 | tf_op jit(solution)/shard_map/ppermute | solution.py:12
  75.0 1.3 collective-permute-start.18
  77.1 3.6 %collective-permute-done.19 = f32[5,1,128]{2,1,0:T(1,128)S(1)} collective-permute-done((f32[5,1,128]{2,1,0:T(1,128)S(1)}, f32[5,1,128]{2,1,0:T(1,128)S(1)}, u32[]{:S(2)}, u32[]{:S(2)}) %collective-permute-start.19) | collective-permute-done | bytes 2592 | tf_op jit(solution)/shard_map/ppermute | solution.py:12
  80.8 1.3 collective-permute-start.24
  82.1 5.7 %collective-permute-start.26 = (f32[5,8,1,128]{3,2,0,1:T(1,128)S(1)}, f32[5,8,1,128]{3,2,0,1:T(1,128)S(1)}, u32[]{:S(2)}, u32[]{:S(2)}) collective-permute-start(f32[5,8,1,128]{3,2,0,1:T(1,128)S(1)} %get-tuple-element.61), channel_id=1, source_target_pairs={{2,0},{4,2},{6,4},{8,6},{10,8},{12,10},{14,12},{16,14},{18,16},{20... | collective-permute-start | bytes 61448 | tf_op jit(solution)/shard_map/ppermute | solution.py:25
  88.4 1.1 collective-permute-done.25
  89.7 5.4 %collective-permute-done.21 = f32[5,9,128]{2,1,0:T(8,128)S(1)} collective-permute-done((f32[5,9,128]{2,1,0:T(8,128)S(1)}, f32[5,9,128]{2,1,0:T(8,128)S(1)}, u32[]{:S(2)}, u32[]{:S(2)}) %collective-permute-start.21) | collective-permute-done | bytes 23072 | tf_op jit(solution)/shard_map/ppermute | solution.py:12
  95.1 6.1 %collective-permute-done.22 = f32[5,9,128]{2,1,0:T(8,128)S(1)} collective-permute-done((f32[5,9,128]{2,1,0:T(8,128)S(1)}, f32[5,9,128]{2,1,0:T(8,128)S(1)}, u32[]{:S(2)}, u32[]{:S(2)}) %collective-permute-start.22) | collective-permute-done | bytes 23072 | tf_op jit(solution)/shard_map/ppermute | solution.py:12
  101.2 4.9 %collective-permute-done.23 = f32[5,9,128]{2,1,0:T(8,128)S(1)} collective-permute-done((f32[5,9,128]{2,1,0:T(8,128)S(1)}, f32[5,9,128]{2,1,0:T(8,128)S(1)}, u32[]{:S(2)}, u32[]{:S(2)}) %collective-permute-start.23) | collective-permute-done | bytes 23072 | tf_op jit(solution)/shard_map/ppermute | solution.py:12
  106.8 1.3 collective-permute-start.27
  109.0 3.6 %collective-permute-done.28 = f32[5,1,128]{2,1,0:T(1,128)S(1)} collective-permute-done((f32[5,1,128]{2,1,0:T(1,128)S(1)}, f32[5,1,128]{2,1,0:T(1,128)S(1)}, u32[]{:S(2)}, u32[]{:S(2)}) %collective-permute-start.28) | collective-permute-done | bytes 2592 | tf_op jit(solution)/shard_map/ppermute | solution.py:12
  112.6 1.3 collective-permute-start.33
  114.0 5.7 %collective-permute-start.35 = (f32[5,8,1,128]{3,2,0,1:T(1,128)S(1)}, f32[5,8,1,128]{3,2,0,1:T(1,128)S(1)}, u32[]{:S(2)}, u32[]{:S(2)}) collective-permute-start(f32[5,8,1,128]{3,2,0,1:T(1,128)S(1)} %get-tuple-element.33), channel_id=1, source_target_pairs={{2,0},{4,2},{6,4},{8,6},{10,8},{12,10},{14,12},{16,14},{18,16},{20... | collective-permute-start | bytes 61448 | tf_op jit(solution)/shard_map/ppermute | solution.py:25
  121.5 5.4 %collective-permute-done.30 = f32[5,9,128]{2,1,0:T(8,128)S(1)} collective-permute-done((f32[5,9,128]{2,1,0:T(8,128)S(1)}, f32[5,9,128]{2,1,0:T(8,128)S(1)}, u32[]{:S(2)}, u32[]{:S(2)}) %collective-permute-start.30) | collective-permute-done | bytes 23072 | tf_op jit(solution)/shard_map/ppermute | solution.py:12
  126.9 6.1 %collective-permute-done.31 = f32[5,9,128]{2,1,0:T(8,128)S(1)} collective-permute-done((f32[5,9,128]{2,1,0:T(8,128)S(1)}, f32[5,9,128]{2,1,0:T(8,128)S(1)}, u32[]{:S(2)}, u32[]{:S(2)}) %collective-permute-start.31) | collective-permute-done | bytes 23072 | tf_op jit(solution)/shard_map/ppermute | solution.py:12
  133.1 4.9 %collective-permute-done.32 = f32[5,9,128]{2,1,0:T(8,128)S(1)} collective-permute-done((f32[5,9,128]{2,1,0:T(8,128)S(1)}, f32[5,9,128]{2,1,0:T(8,128)S(1)}, u32[]{:S(2)}, u32[]{:S(2)}) %collective-permute-start.32) | collective-permute-done | bytes 23072 | tf_op jit(solution)/shard_map/ppermute | solution.py:12
  (122 shorter events, 15.2 us)
Async XLA Ops:
  1.4 12.2 %collective-permute-start = (f32[5,1,8,128]{3,2,0,1:T(8,128)S(1)}, f32[5,1,8,128]{3,2,0,1:T(8,128)S(1)}, u32[]{:S(2)}, u32[]{:S(2)}) collective-permute-start(f32[5,1,8,128]{3,2,0,1:T(8,128)S(1)} %get-tuple-element.108), channel_id=1, source_target_pairs={{0,1},{2,3},{4,5},{6,7},{8,9},{10,11},{12,13},{14,15},{16,17},{18,... | collective-permute-start | bytes 61448 | tf_op jit(solution)/shard_map/ppermute | solution.py:23
  3.8 38.8 %collective-permute-start.6 = (f32[5,1,8,128]{3,2,0,1:T(8,128)S(1)}, f32[5,1,8,128]{3,2,0,1:T(8,128)S(1)}, u32[]{:S(2)}, u32[]{:S(2)}) collective-permute-start(f32[5,1,8,128]{3,2,0,1:T(8,128)S(1)} %get-tuple-element.107), channel_id=1, source_target_pairs={{1,0},{3,2},{5,4},{7,6},{9,8},{11,10},{13,12},{15,14},{17,16},{19,... | collective-permute-start | bytes 61448 | tf_op jit(solution)/shard_map/ppermute | solution.py:25
  6.2 25.5 %collective-permute-start.7 = (f32[5,8,1,128]{3,2,0,1:T(1,128)S(1)}, f32[5,8,1,128]{3,2,0,1:T(1,128)S(1)}, u32[]{:S(2)}, u32[]{:S(2)}) collective-permute-start(f32[5,8,1,128]{3,2,0,1:T(1,128)S(1)} %get-tuple-element.116), channel_id=1, source_target_pairs={{0,2},{2,4},{4,6},{6,8},{8,10},{10,12},{12,14},{14,16},{16,18},{18... | collective-permute-start | bytes 61448 | tf_op jit(solution)/shard_map/ppermute | solution.py:23
  8.5 23.2 %collective-permute-start.8 = (f32[5,8,1,128]{3,2,0,1:T(1,128)S(1)}, f32[5,8,1,128]{3,2,0,1:T(1,128)S(1)}, u32[]{:S(2)}, u32[]{:S(2)}) collective-permute-start(f32[5,8,1,128]{3,2,0,1:T(1,128)S(1)} %get-tuple-element.117), channel_id=1, source_target_pairs={{2,0},{4,2},{6,4},{8,6},{10,8},{12,10},{14,12},{16,14},{18,16},{20... | collective-permute-start | bytes 61448 | tf_op jit(solution)/shard_map/ppermute | solution.py:25
  13.6 3.6 %collective-permute-start.1 = (f32[5,1,128]{2,1,0:T(1,128)S(1)}, f32[5,1,128]{2,1,0:T(1,128)S(1)}, u32[]{:S(2)}, u32[]{:S(2)}) collective-permute-start(f32[5,1,128]{2,1,0:T(1,128)S(1)} %slice.645), channel_id=1, source_target_pairs={{0,30},{2,0},{4,2},{6,4},{8,6},{10,8},{12,10},{14,12},{16,14},{18,... | collective-permute-start | bytes 7688 | tf_op jit(solution)/shard_map/ppermute | solution.py:12
  17.3 7.6 %collective-permute-start.2 = (f32[5,9,128]{2,1,0:T(8,128)S(1)}, f32[5,9,128]{2,1,0:T(8,128)S(1)}, u32[]{:S(2)}, u32[]{:S(2)}) collective-permute-start(f32[5,9,128]{2,1,0:T(8,128)S(1)} %pad_maximum_fusion.8), channel_id=1, source_target_pairs={{0,2},{2,4},{4,6},{6,8},{8,10},{10,12},{12,14},{14,16},{16,18},{18... | collective-permute-start | bytes 69128 | tf_op jit(solution)/shard_map/ppermute | solution.py:12
  24.9 6.7 %collective-permute-start.3 = (f32[5,9,128]{2,1,0:T(8,128)S(1)}, f32[5,9,128]{2,1,0:T(8,128)S(1)}, u32[]{:S(2)}, u32[]{:S(2)}) collective-permute-start(f32[5,9,128]{2,1,0:T(8,128)S(1)} %broadcast_select_fusion.3), channel_id=1, source_target_pairs={{0,4},{2,6},{4,8},{6,10},{8,12},{10,14},{12,16},{14,18},{16,20},{1... | collective-permute-start | bytes 69128 | tf_op jit(solution)/shard_map/ppermute | solution.py:12
  31.6 5.9 %collective-permute-start.4 = (f32[5,9,128]{2,1,0:T(8,128)S(1)}, f32[5,9,128]{2,1,0:T(8,128)S(1)}, u32[]{:S(2)}, u32[]{:S(2)}) collective-permute-start(f32[5,9,128]{2,1,0:T(8,128)S(1)} %broadcast_select_fusion.7), channel_id=1, source_target_pairs={{0,8},{2,10},{4,12},{6,14},{8,16},{10,18},{12,20},{14,22},{16,24},... | collective-permute-start | bytes 69128 | tf_op jit(solution)/shard_map/ppermute | solution.py:12
  37.5 4.9 %collective-permute-start.5 = (f32[5,9,128]{2,1,0:T(8,128)S(1)}, f32[5,9,128]{2,1,0:T(8,128)S(1)}, u32[]{:S(2)}, u32[]{:S(2)}) collective-permute-start(f32[5,9,128]{2,1,0:T(8,128)S(1)} %broadcast_select_fusion.11), channel_id=1, source_target_pairs={{0,16},{2,18},{4,20},{6,22},{8,24},{10,26},{12,28},{14,30},{16,0},... | collective-permute-start | bytes 69128 | tf_op jit(solution)/shard_map/ppermute | solution.py:12
  45.3 3.6 %collective-permute-start.10 = (f32[5,1,128]{2,1,0:T(1,128)S(1)}, f32[5,1,128]{2,1,0:T(1,128)S(1)}, u32[]{:S(2)}, u32[]{:S(2)}) collective-permute-start(f32[5,1,128]{2,1,0:T(1,128)S(1)} %slice.672), channel_id=1, source_target_pairs={{0,30},{2,0},{4,2},{6,4},{8,6},{10,8},{12,10},{14,12},{16,14},{18,... | collective-permute-start | bytes 7688 | tf_op jit(solution)/shard_map/ppermute | solution.py:12
  48.9 7.6 %collective-permute-start.11 = (f32[5,9,128]{2,1,0:T(8,128)S(1)}, f32[5,9,128]{2,1,0:T(8,128)S(1)}, u32[]{:S(2)}, u32[]{:S(2)}) collective-permute-start(f32[5,9,128]{2,1,0:T(8,128)S(1)} %pad_maximum_fusion.9), channel_id=1, source_target_pairs={{0,2},{2,4},{4,6},{6,8},{8,10},{10,12},{12,14},{14,16},{16,18},{18... | collective-permute-start | bytes 69128 | tf_op jit(solution)/shard_map/ppermute | solution.py:12
  48.9 25.6 %collective-permute-start.15 = (f32[5,1,8,128]{3,2,0,1:T(8,128)S(1)}, f32[5,1,8,128]{3,2,0,1:T(8,128)S(1)}, u32[]{:S(2)}, u32[]{:S(2)}) collective-permute-start(f32[5,1,8,128]{3,2,0,1:T(8,128)S(1)} %get-tuple-element.79), channel_id=1, source_target_pairs={{1,0},{3,2},{5,4},{7,6},{9,8},{11,10},{13,12},{15,14},{17,16},{19,... | collective-permute-start | bytes 61448 | tf_op jit(solution)/shard_map/ppermute | solution.py:25
  50.2 7.4 %collective-permute-start.16 = (f32[5,8,1,128]{3,2,0,1:T(1,128)S(1)}, f32[5,8,1,128]{3,2,0,1:T(1,128)S(1)}, u32[]{:S(2)}, u32[]{:S(2)}) collective-permute-start(f32[5,8,1,128]{3,2,0,1:T(1,128)S(1)} %get-tuple-element.88), channel_id=1, source_target_pairs={{0,2},{2,4},{4,6},{6,8},{8,10},{10,12},{12,14},{14,16},{16,18},{18... | collective-permute-start | bytes 61448 | tf_op jit(solution)/shard_map/ppermute | solution.py:23
  50.3 7.4 %collective-permute-start.17 = (f32[5,8,1,128]{3,2,0,1:T(1,128)S(1)}, f32[5,8,1,128]{3,2,0,1:T(1,128)S(1)}, u32[]{:S(2)}, u32[]{:S(2)}) collective-permute-start(f32[5,8,1,128]{3,2,0,1:T(1,128)S(1)} %get-tuple-element.89), channel_id=1, source_target_pairs={{2,0},{4,2},{6,4},{8,6},{10,8},{12,10},{14,12},{16,14},{18,16},{20... | collective-permute-start | bytes 61448 | tf_op jit(solution)/shard_map/ppermute | solution.py:25
  56.5 6.7 %collective-permute-start.12 = (f32[5,9,128]{2,1,0:T(8,128)S(1)}, f32[5,9,128]{2,1,0:T(8,128)S(1)}, u32[]{:S(2)}, u32[]{:S(2)}) collective-permute-start(f32[5,9,128]{2,1,0:T(8,128)S(1)} %broadcast_select_fusion.2), channel_id=1, source_target_pairs={{0,4},{2,6},{4,8},{6,10},{8,12},{10,14},{12,16},{14,18},{16,20},{1... | collective-permute-start | bytes 69128 | tf_op jit(solution)/shard_map/ppermute | solution.py:12
  63.2 6.1 %collective-permute-start.13 = (f32[5,9,128]{2,1,0:T(8,128)S(1)}, f32[5,9,128]{2,1,0:T(8,128)S(1)}, u32[]{:S(2)}, u32[]{:S(2)}) collective-permute-start(f32[5,9,128]{2,1,0:T(8,128)S(1)} %broadcast_select_fusion.6), channel_id=1, source_target_pairs={{0,8},{2,10},{4,12},{6,14},{8,16},{10,18},{12,20},{14,22},{16,24},... | collective-permute-start | bytes 69128 | tf_op jit(solution)/shard_map/ppermute | solution.py:12
  69.4 4.9 %collective-permute-start.14 = (f32[5,9,128]{2,1,0:T(8,128)S(1)}, f32[5,9,128]{2,1,0:T(8,128)S(1)}, u32[]{:S(2)}, u32[]{:S(2)}) collective-permute-start(f32[5,9,128]{2,1,0:T(8,128)S(1)} %broadcast_select_fusion.10), channel_id=1, source_target_pairs={{0,16},{2,18},{4,20},{6,22},{8,24},{10,26},{12,28},{14,30},{16,0},... | collective-permute-start | bytes 69128 | tf_op jit(solution)/shard_map/ppermute | solution.py:12
  77.1 3.6 %collective-permute-start.19 = (f32[5,1,128]{2,1,0:T(1,128)S(1)}, f32[5,1,128]{2,1,0:T(1,128)S(1)}, u32[]{:S(2)}, u32[]{:S(2)}) collective-permute-start(f32[5,1,128]{2,1,0:T(1,128)S(1)} %slice.699), channel_id=1, source_target_pairs={{0,30},{2,0},{4,2},{6,4},{8,6},{10,8},{12,10},{14,12},{16,14},{18,... | collective-permute-start | bytes 7688 | tf_op jit(solution)/shard_map/ppermute | solution.py:12
  80.7 7.6 %collective-permute-start.20 = (f32[5,9,128]{2,1,0:T(8,128)S(1)}, f32[5,9,128]{2,1,0:T(8,128)S(1)}, u32[]{:S(2)}, u32[]{:S(2)}) collective-permute-start(f32[5,9,128]{2,1,0:T(8,128)S(1)} %pad_maximum_fusion.10), channel_id=1, source_target_pairs={{0,2},{2,4},{4,6},{6,8},{8,10},{10,12},{12,14},{14,16},{16,18},{18... | collective-permute-start | bytes 69128 | tf_op jit(solution)/shard_map/ppermute | solution.py:12
  80.8 25.6 %collective-permute-start.24 = (f32[5,1,8,128]{3,2,0,1:T(8,128)S(1)}, f32[5,1,8,128]{3,2,0,1:T(8,128)S(1)}, u32[]{:S(2)}, u32[]{:S(2)}) collective-permute-start(f32[5,1,8,128]{3,2,0,1:T(8,128)S(1)} %get-tuple-element.51), channel_id=1, source_target_pairs={{1,0},{3,2},{5,4},{7,6},{9,8},{11,10},{13,12},{15,14},{17,16},{19,... | collective-permute-start | bytes 61448 | tf_op jit(solution)/shard_map/ppermute | solution.py:25
  82.1 7.4 %collective-permute-start.25 = (f32[5,8,1,128]{3,2,0,1:T(1,128)S(1)}, f32[5,8,1,128]{3,2,0,1:T(1,128)S(1)}, u32[]{:S(2)}, u32[]{:S(2)}) collective-permute-start(f32[5,8,1,128]{3,2,0,1:T(1,128)S(1)} %get-tuple-element.60), channel_id=1, source_target_pairs={{0,2},{2,4},{4,6},{6,8},{8,10},{10,12},{12,14},{14,16},{16,18},{18... | collective-permute-start | bytes 61448 | tf_op jit(solution)/shard_map/ppermute | solution.py:23
  82.1 7.4 %collective-permute-start.26 = (f32[5,8,1,128]{3,2,0,1:T(1,128)S(1)}, f32[5,8,1,128]{3,2,0,1:T(1,128)S(1)}, u32[]{:S(2)}, u32[]{:S(2)}) collective-permute-start(f32[5,8,1,128]{3,2,0,1:T(1,128)S(1)} %get-tuple-element.61), channel_id=1, source_target_pairs={{2,0},{4,2},{6,4},{8,6},{10,8},{12,10},{14,12},{16,14},{18,16},{20... | collective-permute-start | bytes 61448 | tf_op jit(solution)/shard_map/ppermute | solution.py:25
  88.3 6.7 %collective-permute-start.21 = (f32[5,9,128]{2,1,0:T(8,128)S(1)}, f32[5,9,128]{2,1,0:T(8,128)S(1)}, u32[]{:S(2)}, u32[]{:S(2)}) collective-permute-start(f32[5,9,128]{2,1,0:T(8,128)S(1)} %broadcast_select_fusion.1), channel_id=1, source_target_pairs={{0,4},{2,6},{4,8},{6,10},{8,12},{10,14},{12,16},{14,18},{16,20},{1... | collective-permute-start | bytes 69128 | tf_op jit(solution)/shard_map/ppermute | solution.py:12
  95.1 6.1 %collective-permute-start.22 = (f32[5,9,128]{2,1,0:T(8,128)S(1)}, f32[5,9,128]{2,1,0:T(8,128)S(1)}, u32[]{:S(2)}, u32[]{:S(2)}) collective-permute-start(f32[5,9,128]{2,1,0:T(8,128)S(1)} %broadcast_select_fusion.5), channel_id=1, source_target_pairs={{0,8},{2,10},{4,12},{6,14},{8,16},{10,18},{12,20},{14,22},{16,24},... | collective-permute-start | bytes 69128 | tf_op jit(solution)/shard_map/ppermute | solution.py:12
  101.2 4.9 %collective-permute-start.23 = (f32[5,9,128]{2,1,0:T(8,128)S(1)}, f32[5,9,128]{2,1,0:T(8,128)S(1)}, u32[]{:S(2)}, u32[]{:S(2)}) collective-permute-start(f32[5,9,128]{2,1,0:T(8,128)S(1)} %broadcast_select_fusion.9), channel_id=1, source_target_pairs={{0,16},{2,18},{4,20},{6,22},{8,24},{10,26},{12,28},{14,30},{16,0},... | collective-permute-start | bytes 69128 | tf_op jit(solution)/shard_map/ppermute | solution.py:12
  112.5 7.6 %collective-permute-start.29 = (f32[5,9,128]{2,1,0:T(8,128)S(1)}, f32[5,9,128]{2,1,0:T(8,128)S(1)}, u32[]{:S(2)}, u32[]{:S(2)}) collective-permute-start(f32[5,9,128]{2,1,0:T(8,128)S(1)} %pad_maximum_fusion.11), channel_id=1, source_target_pairs={{0,2},{2,4},{4,6},{6,8},{8,10},{10,12},{12,14},{14,16},{16,18},{18... | collective-permute-start | bytes 69128 | tf_op jit(solution)/shard_map/ppermute | solution.py:12
  112.6 25.6 %collective-permute-start.33 = (f32[5,1,8,128]{3,2,0,1:T(8,128)S(1)}, f32[5,1,8,128]{3,2,0,1:T(8,128)S(1)}, u32[]{:S(2)}, u32[]{:S(2)}) collective-permute-start(f32[5,1,8,128]{3,2,0,1:T(8,128)S(1)} %get-tuple-element.23), channel_id=1, source_target_pairs={{1,0},{3,2},{5,4},{7,6},{9,8},{11,10},{13,12},{15,14},{17,16},{19,... | collective-permute-start | bytes 61448 | tf_op jit(solution)/shard_map/ppermute | solution.py:25
  113.9 7.4 %collective-permute-start.34 = (f32[5,8,1,128]{3,2,0,1:T(1,128)S(1)}, f32[5,8,1,128]{3,2,0,1:T(1,128)S(1)}, u32[]{:S(2)}, u32[]{:S(2)}) collective-permute-start(f32[5,8,1,128]{3,2,0,1:T(1,128)S(1)} %get-tuple-element.32), channel_id=1, source_target_pairs={{0,2},{2,4},{4,6},{6,8},{8,10},{10,12},{12,14},{14,16},{16,18},{18... | collective-permute-start | bytes 61448 | tf_op jit(solution)/shard_map/ppermute | solution.py:23
  114.0 7.4 %collective-permute-start.35 = (f32[5,8,1,128]{3,2,0,1:T(1,128)S(1)}, f32[5,8,1,128]{3,2,0,1:T(1,128)S(1)}, u32[]{:S(2)}, u32[]{:S(2)}) collective-permute-start(f32[5,8,1,128]{3,2,0,1:T(1,128)S(1)} %get-tuple-element.33), channel_id=1, source_target_pairs={{2,0},{4,2},{6,4},{8,6},{10,8},{12,10},{14,12},{16,14},{18,16},{20... | collective-permute-start | bytes 61448 | tf_op jit(solution)/shard_map/ppermute | solution.py:25
  120.2 6.7 %collective-permute-start.30 = (f32[5,9,128]{2,1,0:T(8,128)S(1)}, f32[5,9,128]{2,1,0:T(8,128)S(1)}, u32[]{:S(2)}, u32[]{:S(2)}) collective-permute-start(f32[5,9,128]{2,1,0:T(8,128)S(1)} %broadcast_select_fusion), channel_id=1, source_target_pairs={{0,4},{2,6},{4,8},{6,10},{8,12},{10,14},{12,16},{14,18},{16,20},{1... | collective-permute-start | bytes 69128 | tf_op jit(solution)/shard_map/ppermute | solution.py:12
  126.9 6.1 %collective-permute-start.31 = (f32[5,9,128]{2,1,0:T(8,128)S(1)}, f32[5,9,128]{2,1,0:T(8,128)S(1)}, u32[]{:S(2)}, u32[]{:S(2)}) collective-permute-start(f32[5,9,128]{2,1,0:T(8,128)S(1)} %broadcast_select_fusion.4), channel_id=1, source_target_pairs={{0,8},{2,10},{4,12},{6,14},{8,16},{10,18},{12,20},{14,22},{16,24},... | collective-permute-start | bytes 69128 | tf_op jit(solution)/shard_map/ppermute | solution.py:12
  133.0 4.9 %collective-permute-start.32 = (f32[5,9,128]{2,1,0:T(8,128)S(1)}, f32[5,9,128]{2,1,0:T(8,128)S(1)}, u32[]{:S(2)}, u32[]{:S(2)}) collective-permute-start(f32[5,9,128]{2,1,0:T(8,128)S(1)} %broadcast_select_fusion.8), channel_id=1, source_target_pairs={{0,16},{2,18},{4,20},{6,22},{8,24},{10,26},{12,28},{14,30},{16,0},... | collective-permute-start | bytes 69128 | tf_op jit(solution)/shard_map/ppermute | solution.py:12
  (9 other events, 104.2 us)
where the time goes:
time: 140 us
  waiting for transfers between devices  91.8 us (66%)
  starting transfers between devices  37.3 us (27%)
  local copies, waits for them, and re-layouts  5.66 us (4%)
  other arithmetic  2.37 us (2%)
  between operations  1.96 us (1%)
    ppermute x20, waiting for transfers between devices, passed_along(): return lax.ppermute(value, axis, pairs)  86 us
    ppermute x8, starting transfers between devices, padded(): lax.ppermute(head, axis, [((i + 1) % count, i) for i in range(ends)])  26.2 us
    ppermute x8, starting transfers between devices, padded(): lax.ppermute(tail, axis, [(i, (i + 1) % count) for i in range(ends)])  8.8 us
    ppermute x8, waiting for transfers between devices, padded(): lax.ppermute(tail, axis, [(i, (i + 1) % count) for i in range(ends)])  5.8 us
  transfers between devices with their start and end apart: 36, of which 26 were waited for; matrix products, arithmetic and copies ran while one was open for 4% of the time, Pallas kernels for 0%

commit v1 on v0

v1 whole, which is shorter than its diff:
```python
import jax
import jax.numpy as jnp
from jax import lax
from jax.sharding import PartitionSpec as P

ITERS = 4
AXES = ("sector", "block")


def solution(mesh):
    sectors, blocks = mesh.shape["sector"], mesh.shape["block"]
    half = blocks // 2

    def at(s, b):
        return (s % sectors) * blocks + b

    def around(step):
        return [(at(s, b), at(s + step, b)) for s in range(sectors) for b in range(blocks)]

    from_above = [(at(s, b), at(s, b - 1)) for s in range(sectors) for b in range(1, blocks)]

    def from_below(offset):
        return [
            (at(s, b), at(s + (offset if b + 1 == half else 0), b + 1))
            for s in range(sectors)
            for b in range(blocks - 1)
        ]

    def axial_exchange(first, last, offset, block_index):
        if blocks == 2:
            sent = jnp.where(block_index == 0, last, first)
            got = lax.ppermute(sent, AXES, from_above + from_below(offset))
            zero = jnp.zeros_like(got)
            return got, jnp.where(block_index == 0, zero, got), jnp.where(block_index == 0, got, zero)
        below = lax.ppermute(last, AXES, from_below(offset))
        return below, below, lax.ppermute(first, AXES, from_above)

    def sweeps(offset, adjoint, source, face, inverse, table):
        block_index = lax.axis_index("block")
        layers, cells = adjoint.shape[1], adjoint.shape[2]

        def sweep(_, carry):
            adjoint, _ = carry
            row, below, above = axial_exchange(adjoint[:, 0], adjoint[:, -1], offset, block_index)
            minus = lax.ppermute(adjoint[:, :, -1], AXES, around(1))
            head = jnp.concatenate([adjoint[:, :, 0], row[:, :1]], axis=1)
            plus = lax.ppermute(head, AXES, around(-1))
            facing_row = jnp.concatenate([row, plus[:, layers:]], axis=1)
            facing = jnp.einsum("jk,nkr->njr", table, facing_row, precision=lax.Precision.HIGHEST)
            below = jnp.where(block_index == half, facing, below)
            axial_minus = jnp.concatenate([below[:, None], adjoint[:, :-1]], axis=1)
            axial_plus = jnp.concatenate([adjoint[:, 1:], above[:, None]], axis=1)
            around_minus = jnp.concatenate([minus[:, :, None], adjoint[:, :, :-1]], axis=2)
            around_plus = jnp.concatenate([adjoint[:, :, 1:], plus[:, :layers, None]], axis=2)
            radial = jnp.pad(adjoint, ((0, 0), (0, 0), (0, 0), (1, 1)))
            mixed = (
                0.6 * axial_minus + 0.4 * axial_plus,
                0.6 * around_minus + 0.4 * around_plus,
                0.6 * radial[:, :, :, :-2] + 0.4 * radial[:, :, :, 2:],
            )
            total = source
            for direction in range(3):
                for comp in range(5):
                    total = total + face[direction, comp].astype(jnp.float32) * mixed[direction][comp][None]
            result = jnp.zeros_like(adjoint)
            for comp in range(5):
                result = result + inverse[:, comp].astype(jnp.float32) * total[comp][None]
            return result, adjoint

        adjoint, previous = lax.fori_loop(0, ITERS, sweep, (adjoint, adjoint))
        return adjoint, adjoint - previous

    def shards(adjoint_prev, adjoint_source, face, inverse, sector_offset, donor_cells, donor_weights):
        columns = jnp.arange(adjoint_prev.shape[2] + 1, dtype=jnp.int32)
        first_hit = (columns[None, :] == donor_cells[:, None]).astype(jnp.float32)
        second_hit = (columns[None, :] == donor_cells[:, None] + 1).astype(jnp.float32)
        table = donor_weights[:, None] * first_hit + (1.0 - donor_weights[:, None]) * second_hit
        branches = [
            lambda *args, offset=offset: sweeps(offset, *args) for offset in range(1, sectors)
        ]
        return lax.switch(
            sector_offset[0] - 1, branches, adjoint_prev, adjoint_source, face, inverse, table
        )

    return jax.shard_map(
        shards,
        mesh=mesh,
        in_specs=(
            P(None, "block", "sector", None),
            P(None, "block", "sector", None),
            P(None, None, None, "block", "sector", None),
            P(None, None, "block", "sector", None),
            P(),
            P("sector"),
            P("sector"),
        ),
        out_specs=(P(None, "block", "sector", None), P(None, "block", "sector", None)),
        check_vma=False,
    )
```

time: 140 us -> 79.4 us (0.57)
  waiting for transfers between devices: 91.8 us -> 6.7 us
  local copies, waits for them, and re-layouts: 5.66 us -> 25.8 us
  other arithmetic: 2.37 us -> 16.1 us
  starting transfers between devices: 37.3 us -> 27.3 us
    ppermute x36 -> x12, waiting for transfers between devices: 91.8 us -> 6.7 us  [the longest x4 6.68 us: sweep(): plus = lax.ppermute(head, AXES, around(-1))]
    another operation x0 -> x8, local copies, waits for them, and re-layouts: none -> 10.6 us
    ppermute x36 -> x12, starting transfers between devices: 37.3 us -> 27.3 us  [the longest x4 21.5 us: sweep(): plus = lax.ppermute(head, AXES, around(-1))]
    add x15 -> x21, other arithmetic: 2.17 us -> 9.97 us  [the longest x4 4.57 us: sweep(): 0.6 * radial[:, :, :, :-2] + 0.4 * radial[:, :, :, 2:]]
    slice x17 -> x20, local copies, waits for them, and re-layouts: 4.05 us -> 8.16 us  [the longest x4 4.08 us: sweep(): adjoint[:, :, 1:]]
    while x0 -> x25, local copies, waits for them, and re-layouts: none -> 3.39 us
    select_n x12 -> x4, other arithmetic: 0.08 us -> 3.05 us  [axial_exchange(): sent = jnp.where(block_index == 0, last, first)]
    cond x0 -> x3, local copies, waits for them, and re-layouts: none -> 2.5 us
  transfers between devices with their start and end apart: 36 -> 12, of which waited for: 26 -> 4; matrix products, arithmetic and copies ran while one was open for 4% -> 31% of each run, Pallas kernels for 0% -> 0%
where the time goes in v1:
time: 79.4 us; the launch traced here: 78.4 us
  starting transfers between devices  27.3 us (34%)
  local copies, waits for them, and re-layouts  25.8 us (32%)
  other arithmetic  16.1 us (20%)
  waiting for transfers between devices  6.7 us (8%)
  between operations  1.29 us (2%)
    ppermute x4, starting transfers between devices, sweep(): plus = lax.ppermute(head, AXES, around(-1))  21.5 us
    another operation x8, local copies, waits for them, and re-layouts  10.6 us
    ppermute x4, waiting for transfers between devices, sweep(): plus = lax.ppermute(head, AXES, around(-1))  6.68 us
    add x4, other arithmetic, sweep(): 0.6 * radial[:, :, :, :-2] + 0.4 * radial[:, :, :, 2:]  4.57 us
    slice x4, local copies, waits for them, and re-layouts, sweep(): adjoint[:, :, 1:]  4.08 us
    slice x4, local copies, waits for them, and re-layouts, sweep(): axial_plus = jnp.concatenate([adjoint[:, 1:], above[:, None]], axis=1)  4.05 us
    ppermute x4, starting transfers between devices, axial_exchange(): got = lax.ppermute(sent, AXES, from_above + from_below(offset))  3.51 us
    select_n x4, other arithmetic, axial_exchange(): sent = jnp.where(block_index == 0, last, first)  3.05 us
  transfers between devices with their start and end apart: 12, of which 4 were waited for; matrix products, arithmetic and copies ran while one was open for 31% of the time, Pallas kernels for 0%

profile of v1, /device:TPU:0, one launch (start us, length us, event | category | flops | bytes accessed | tf_op | source)
XLA Modules:
  0.0 78.4 jit_solution(12791227000460155459)
XLA Ops:
  4.3 72.5 %conditional.1 = (f32[5,8,8,128]{3,2,1,0:T(8,128)S(1)}, f32[5,8,8,128]{3,2,1,0:T(8,128)}, (s32[]{:T(128)}, f32[5,8,8,128]{3,2,1,0:T(8,128)S(1)}, f32[5,8,8,128]{...) conditional(s32[]{:T(128)} %bitcast.780, ...), branch_computations={%region_0.3_spmd, %region_3.6_spmd, %region_6.9_spmd, %region_9.12... | conditional | flops 3534086 | bytes 16311090 | solution.py:81
  5.6 69.3 %while.202 = (s32[]{:T(128)}, f32[5,8,8,128]{3,2,1,0:T(8,128)}, f32[5,8,8,128]{3,2,0,1:T(8,128)}, bf16[5,5,8,8,128]{4,3,2,1,0:T(8,128)(2,1)}, bf16[3,5,5,8,8,128...) while((s32[]{:T(128)}, f32[5,8,8,128]{3,2,1,0:T(8,128)}, ...), condition=%wide.region_23.23_spmd, body=%wide.region_22.22_spmd.sunk | while | flops 3534082 | bytes 15000148 | solution.py:70
  6.4 3.5 %collective-permute-start.22 = (f32[5,8,128]{2,1,0:T(8,128)S(1)}, f32[5,8,128]{2,1,0:T(8,128)S(1)}, u32[]{:S(2)}, u32[]{:S(2)}) collective-permute-start(f32[5,8,128]{2,1,0:T(8,128)S(1)} %fusion.832), channel_id=1, source_target_pairs={{1,0},{3,2},{5,4},{7,6},{9,8},{11,10},{13,12},{15,14},{17,16},{19,... | collective-permute-start | bytes 61448 | tf_op jit(solution)/shard_map/cond/branch_7_fun/while/body/eval_jaxpr/ppermute | solution.py:32
  10.8 1.5 %collective-permute-start.21 = (f32[5,8,128]{2,1,0:T(8,128)S(1)}, f32[5,8,128]{2,1,0:T(8,128)S(1)}, u32[]{:S(2)}, u32[]{:S(2)}) collective-permute-start(f32[5,8,128]{2,1,0:T(8,128)S(1)} %get-tuple-element.4128), channel_id=1, source_target_pairs={{0,2},{1,3},{2,4},{3,5},{4,6},{5,7},{6,8},{7,9},{8,10},{9,11},{10,... | collective-permute-start | bytes 61448 | tf_op jit(solution)/shard_map/cond/branch_7_fun/while/body/eval_jaxpr/ppermute | solution.py:45
  12.4 1.1 %fusion.830 = f32[5,8,8,128]{3,2,1,0:T(8,128)S(1)} fusion(f32[5,8,8,128]{3,2,1,0:T(8,128)} %get-tuple-element.4607), kind=kLoop, calls=%fused_computation.629.clone.1 | loop fusion | flops 122880 | bytes 327680 | tf_op jit(solution)/shard_map/cond/branch_7_fun/while/body/eval_jaxpr/add | solution.py:59
  13.5 1.0 %fusion.834 = (f32[5,7,8,128]{3,2,1,0:T(8,128)S(1)}, f32[5,7,8,128]{3,2,1,0:T(8,128)S(1)}) fusion(f32[5,8,8,128]{3,2,1,0:T(8,128)} %get-tuple-element.4607), kind=kLoop, calls=%fused_computation.1355.clone.1 | loop fusion | bytes 573440 | tf_op jit(solution)/shard_map/cond/branch_7_fun/while/body/eval_jaxpr/slice | solution.py:52
  14.6 1.0 %fusion.831 = (f32[5,8,7,128]{3,2,1,0:T(8,128)S(1)}, f32[5,8,7,128]{3,2,1,0:T(8,128)S(1)}) fusion(f32[5,8,8,128]{3,2,1,0:T(8,128)} %get-tuple-element.4607), kind=kLoop, calls=%fused_computation.1356.clone.1 | loop fusion | bytes 573440 | tf_op jit(solution)/shard_map/cond/branch_7_fun/while/body/eval_jaxpr/slice | solution.py:54
  15.6 1.7 %copy.372 = f32[5,8,8,128]{3,2,0,1:T(8,128)} copy(f32[5,8,8,128]{3,2,1,0:T(8,128)} %get-tuple-element.4607) | data formatting | bytes 327680 | tf_op jit(solution)/shard_map
  17.3 4.2 %collective-permute-start.23 = (f32[5,9,128]{2,1,0:T(8,128)S(1)}, f32[5,9,128]{2,1,0:T(8,128)S(1)}, u32[]{:S(2)}, u32[]{:S(2)}) collective-permute-start(f32[5,9,128]{2,1,0:T(8,128)S(1)} %pad_maximum_fusion.37), channel_id=1, source_target_pairs={{0,30},{1,31},{2,0},{3,1},{4,2},{5,3},{6,4},{7,5},{8,6},{9,7},{10,... | collective-permute-start | bytes 69128 | tf_op jit(solution)/shard_map/cond/branch_7_fun/while/body/eval_jaxpr/ppermute | solution.py:47
  21.5 1.7 %collective-permute-done.23 = f32[5,9,128]{2,1,0:T(8,128)S(1)} collective-permute-done((f32[5,9,128]{2,1,0:T(8,128)S(1)}, f32[5,9,128]{2,1,0:T(8,128)S(1)}, u32[]{:S(2)}, u32[]{:S(2)}) %collective-permute-start.23) | collective-permute-done | bytes 23072 | tf_op jit(solution)/shard_map/cond/branch_7_fun/while/body/eval_jaxpr/ppermute | solution.py:47
  26.1 0.9 %copy.371 = f32[5,8,8,128]{3,1,0,2:T(8,128)S(1)} copy(f32[5,8,8,128]{3,2,1,0:T(8,128)} %get-tuple-element.4607) | data formatting | bytes 327680 | tf_op jit(solution)/shard_map
  27.7 1.1 %fusion.830 = f32[5,8,8,128]{3,2,1,0:T(8,128)S(1)} fusion(f32[5,8,8,128]{3,2,1,0:T(8,128)} %get-tuple-element.4607), kind=kLoop, calls=%fused_computation.629.clone.1 | loop fusion | flops 122880 | bytes 327680 | tf_op jit(solution)/shard_map/cond/branch_7_fun/while/body/eval_jaxpr/add | solution.py:59
  28.8 1.0 %fusion.834 = (f32[5,7,8,128]{3,2,1,0:T(8,128)S(1)}, f32[5,7,8,128]{3,2,1,0:T(8,128)S(1)}) fusion(f32[5,8,8,128]{3,2,1,0:T(8,128)} %get-tuple-element.4607), kind=kLoop, calls=%fused_computation.1355.clone.1 | loop fusion | bytes 573440 | tf_op jit(solution)/shard_map/cond/branch_7_fun/while/body/eval_jaxpr/slice | solution.py:52
  29.9 1.0 %fusion.831 = (f32[5,8,7,128]{3,2,1,0:T(8,128)S(1)}, f32[5,8,7,128]{3,2,1,0:T(8,128)S(1)}) fusion(f32[5,8,8,128]{3,2,1,0:T(8,128)} %get-tuple-element.4607), kind=kLoop, calls=%fused_computation.1356.clone.1 | loop fusion | bytes 573440 | tf_op jit(solution)/shard_map/cond/branch_7_fun/while/body/eval_jaxpr/slice | solution.py:54
  30.9 1.7 %copy.372 = f32[5,8,8,128]{3,2,0,1:T(8,128)} copy(f32[5,8,8,128]{3,2,1,0:T(8,128)} %get-tuple-element.4607) | data formatting | bytes 327680 | tf_op jit(solution)/shard_map
  32.6 5.4 %collective-permute-start.23 = (f32[5,9,128]{2,1,0:T(8,128)S(1)}, f32[5,9,128]{2,1,0:T(8,128)S(1)}, u32[]{:S(2)}, u32[]{:S(2)}) collective-permute-start(f32[5,9,128]{2,1,0:T(8,128)S(1)} %pad_maximum_fusion.37), channel_id=1, source_target_pairs={{0,30},{1,31},{2,0},{3,1},{4,2},{5,3},{6,4},{7,5},{8,6},{9,7},{10,... | collective-permute-start | bytes 69128 | tf_op jit(solution)/shard_map/cond/branch_7_fun/while/body/eval_jaxpr/ppermute | solution.py:47
  38.1 1.7 %collective-permute-done.23 = f32[5,9,128]{2,1,0:T(8,128)S(1)} collective-permute-done((f32[5,9,128]{2,1,0:T(8,128)S(1)}, f32[5,9,128]{2,1,0:T(8,128)S(1)}, u32[]{:S(2)}, u32[]{:S(2)}) %collective-permute-start.23) | collective-permute-done | bytes 23072 | tf_op jit(solution)/shard_map/cond/branch_7_fun/while/body/eval_jaxpr/ppermute | solution.py:47
  42.6 0.9 %copy.371 = f32[5,8,8,128]{3,1,0,2:T(8,128)S(1)} copy(f32[5,8,8,128]{3,2,1,0:T(8,128)} %get-tuple-element.4607) | data formatting | bytes 327680 | tf_op jit(solution)/shard_map
  43.6 1.1 %fusion.830 = f32[5,8,8,128]{3,2,1,0:T(8,128)S(1)} fusion(f32[5,8,8,128]{3,2,1,0:T(8,128)} %get-tuple-element.4607), kind=kLoop, calls=%fused_computation.629.clone.1 | loop fusion | flops 122880 | bytes 327680 | tf_op jit(solution)/shard_map/cond/branch_7_fun/while/body/eval_jaxpr/add | solution.py:59
  44.8 1.0 %fusion.834 = (f32[5,7,8,128]{3,2,1,0:T(8,128)S(1)}, f32[5,7,8,128]{3,2,1,0:T(8,128)S(1)}) fusion(f32[5,8,8,128]{3,2,1,0:T(8,128)} %get-tuple-element.4607), kind=kLoop, calls=%fused_computation.1355.clone.1 | loop fusion | bytes 573440 | tf_op jit(solution)/shard_map/cond/branch_7_fun/while/body/eval_jaxpr/slice | solution.py:52
  45.8 1.0 %fusion.831 = (f32[5,8,7,128]{3,2,1,0:T(8,128)S(1)}, f32[5,8,7,128]{3,2,1,0:T(8,128)S(1)}) fusion(f32[5,8,8,128]{3,2,1,0:T(8,128)} %get-tuple-element.4607), kind=kLoop, calls=%fused_computation.1356.clone.1 | loop fusion | bytes 573440 | tf_op jit(solution)/shard_map/cond/branch_7_fun/while/body/eval_jaxpr/slice | solution.py:54
  46.9 1.7 %copy.372 = f32[5,8,8,128]{3,2,0,1:T(8,128)} copy(f32[5,8,8,128]{3,2,1,0:T(8,128)} %get-tuple-element.4607) | data formatting | bytes 327680 | tf_op jit(solution)/shard_map
  48.6 6.0 %collective-permute-start.23 = (f32[5,9,128]{2,1,0:T(8,128)S(1)}, f32[5,9,128]{2,1,0:T(8,128)S(1)}, u32[]{:S(2)}, u32[]{:S(2)}) collective-permute-start(f32[5,9,128]{2,1,0:T(8,128)S(1)} %pad_maximum_fusion.37), channel_id=1, source_target_pairs={{0,30},{1,31},{2,0},{3,1},{4,2},{5,3},{6,4},{7,5},{8,6},{9,7},{10,... | collective-permute-start | bytes 69128 | tf_op jit(solution)/shard_map/cond/branch_7_fun/while/body/eval_jaxpr/ppermute | solution.py:47
  54.6 1.7 %collective-permute-done.23 = f32[5,9,128]{2,1,0:T(8,128)S(1)} collective-permute-done((f32[5,9,128]{2,1,0:T(8,128)S(1)}, f32[5,9,128]{2,1,0:T(8,128)S(1)}, u32[]{:S(2)}, u32[]{:S(2)}) %collective-permute-start.23) | collective-permute-done | bytes 23072 | tf_op jit(solution)/shard_map/cond/branch_7_fun/while/body/eval_jaxpr/ppermute | solution.py:47
  59.1 0.9 %copy.371 = f32[5,8,8,128]{3,1,0,2:T(8,128)S(1)} copy(f32[5,8,8,128]{3,2,1,0:T(8,128)} %get-tuple-element.4607) | data formatting | bytes 327680 | tf_op jit(solution)/shard_map
  60.2 1.1 %fusion.830 = f32[5,8,8,128]{3,2,1,0:T(8,128)S(1)} fusion(f32[5,8,8,128]{3,2,1,0:T(8,128)} %get-tuple-element.4607), kind=kLoop, calls=%fused_computation.629.clone.1 | loop fusion | flops 122880 | bytes 327680 | tf_op jit(solution)/shard_map/cond/branch_7_fun/while/body/eval_jaxpr/add | solution.py:59
  61.3 1.0 %fusion.834 = (f32[5,7,8,128]{3,2,1,0:T(8,128)S(1)}, f32[5,7,8,128]{3,2,1,0:T(8,128)S(1)}) fusion(f32[5,8,8,128]{3,2,1,0:T(8,128)} %get-tuple-element.4607), kind=kLoop, calls=%fused_computation.1355.clone.1 | loop fusion | bytes 573440 | tf_op jit(solution)/shard_map/cond/branch_7_fun/while/body/eval_jaxpr/slice | solution.py:52
  62.3 1.0 %fusion.831 = (f32[5,8,7,128]{3,2,1,0:T(8,128)S(1)}, f32[5,8,7,128]{3,2,1,0:T(8,128)S(1)}) fusion(f32[5,8,8,128]{3,2,1,0:T(8,128)} %get-tuple-element.4607), kind=kLoop, calls=%fused_computation.1356.clone.1 | loop fusion | bytes 573440 | tf_op jit(solution)/shard_map/cond/branch_7_fun/while/body/eval_jaxpr/slice | solution.py:54
  63.4 1.7 %copy.372 = f32[5,8,8,128]{3,2,0,1:T(8,128)} copy(f32[5,8,8,128]{3,2,1,0:T(8,128)} %get-tuple-element.4607) | data formatting | bytes 327680 | tf_op jit(solution)/shard_map
  65.1 6.0 %collective-permute-start.23 = (f32[5,9,128]{2,1,0:T(8,128)S(1)}, f32[5,9,128]{2,1,0:T(8,128)S(1)}, u32[]{:S(2)}, u32[]{:S(2)}) collective-permute-start(f32[5,9,128]{2,1,0:T(8,128)S(1)} %pad_maximum_fusion.37), channel_id=1, source_target_pairs={{0,30},{1,31},{2,0},{3,1},{4,2},{5,3},{6,4},{7,5},{8,6},{9,7},{10,... | collective-permute-start | bytes 69128 | tf_op jit(solution)/shard_map/cond/branch_7_fun/while/body/eval_jaxpr/ppermute | solution.py:47
  71.1 1.7 %collective-permute-done.23 = f32[5,9,128]{2,1,0:T(8,128)S(1)} collective-permute-done((f32[5,9,128]{2,1,0:T(8,128)S(1)}, f32[5,9,128]{2,1,0:T(8,128)S(1)}, u32[]{:S(2)}, u32[]{:S(2)}) %collective-permute-start.23) | collective-permute-done | bytes 23072 | tf_op jit(solution)/shard_map/cond/branch_7_fun/while/body/eval_jaxpr/ppermute | solution.py:47
  76.7 1.7 %copy_subtract_fusion = f32[5,8,8,128]{3,2,1,0:T(8,128)} fusion(f32[5,8,8,128]{3,2,1,0:T(8,128)} %get-tuple-element.1803, f32[5,8,8,128]{3,2,0,1:T(8,128)} %get-tuple-element.1805), kind=kLoop, calls=%fused_computation.1335 | loop fusion | flops 40960 | bytes 491520 | tf_op jit(solution)/shard_map/cond/branch_0_fun/sub | solution.py:71
  (107 shorter events, 19.3 us)
Async XLA Ops:
  6.4 10.9 %collective-permute-start.22 = (f32[5,8,128]{2,1,0:T(8,128)S(1)}, f32[5,8,128]{2,1,0:T(8,128)S(1)}, u32[]{:S(2)}, u32[]{:S(2)}) collective-permute-start(f32[5,8,128]{2,1,0:T(8,128)S(1)} %fusion.832), channel_id=1, source_target_pairs={{1,0},{3,2},{5,4},{7,6},{9,8},{11,10},{13,12},{15,14},{17,16},{19,... | collective-permute-start | bytes 61448 | tf_op jit(solution)/shard_map/cond/branch_7_fun/while/body/eval_jaxpr/ppermute | solution.py:32
  10.8 12.6 %collective-permute-start.21 = (f32[5,8,128]{2,1,0:T(8,128)S(1)}, f32[5,8,128]{2,1,0:T(8,128)S(1)}, u32[]{:S(2)}, u32[]{:S(2)}) collective-permute-start(f32[5,8,128]{2,1,0:T(8,128)S(1)} %get-tuple-element.4128), channel_id=1, source_target_pairs={{0,2},{1,3},{2,4},{3,5},{4,6},{5,7},{6,8},{7,9},{8,10},{9,11},{10,... | collective-permute-start | bytes 61448 | tf_op jit(solution)/shard_map/cond/branch_7_fun/while/body/eval_jaxpr/ppermute | solution.py:45
  15.6 8.0 %copy-start.7 = (bf16[3,5,5,8,8,128]{5,4,3,2,1,0:T(8,128)(2,1)S(1)}, bf16[3,5,5,8,8,128]{5,4,3,2,1,0:T(8,128)(2,1)}, u32[]{:S(2)}) copy-start(bf16[3,5,5,8,8,128]{5,4,3,2,1,0:T(8,128)(2,1)} %get-tuple-element.4620) | copy-start | bytes 3686404 | tf_op jit(solution)/shard_map/cond/branch_7_fun/while
  15.6 8.0 %copy-start.37 = (f32[5,8,8,128]{3,2,1,0:T(8,128)S(1)}, f32[5,8,8,128]{3,2,1,0:T(8,128)}, u32[]{:S(2)}) copy-start(f32[5,8,8,128]{3,2,1,0:T(8,128)} %get-tuple-element.4624) | copy-start | bytes 491524 | tf_op jit(solution)/shard_map/cond/branch_7_fun/while
  17.3 5.9 %collective-permute-start.23 = (f32[5,9,128]{2,1,0:T(8,128)S(1)}, f32[5,9,128]{2,1,0:T(8,128)S(1)}, u32[]{:S(2)}, u32[]{:S(2)}) collective-permute-start(f32[5,9,128]{2,1,0:T(8,128)S(1)} %pad_maximum_fusion.37), channel_id=1, source_target_pairs={{0,30},{1,31},{2,0},{3,1},{4,2},{5,3},{6,4},{7,5},{8,6},{9,7},{10,... | collective-permute-start | bytes 69128 | tf_op jit(solution)/shard_map/cond/branch_7_fun/while/body/eval_jaxpr/ppermute | solution.py:47
  23.6 1.0 %copy-start.22 = (bf16[5,5,8,8,128]{4,3,2,1,0:T(8,128)(2,1)S(1)}, bf16[5,5,8,8,128]{4,3,2,1,0:T(8,128)(2,1)}, u32[]{:S(2)}) copy-start(bf16[5,5,8,8,128]{4,3,2,1,0:T(8,128)(2,1)} %get-tuple-element.4619) | copy-start | bytes 1228804 | tf_op jit(solution)/shard_map/cond/branch_7_fun/while
  26.1 6.5 %collective-permute-start.22 = (f32[5,8,128]{2,1,0:T(8,128)S(1)}, f32[5,8,128]{2,1,0:T(8,128)S(1)}, u32[]{:S(2)}, u32[]{:S(2)}) collective-permute-start(f32[5,8,128]{2,1,0:T(8,128)S(1)} %fusion.832), channel_id=1, source_target_pairs={{1,0},{3,2},{5,4},{7,6},{9,8},{11,10},{13,12},{15,14},{17,16},{19,... | collective-permute-start | bytes 61448 | tf_op jit(solution)/shard_map/cond/branch_7_fun/while/body/eval_jaxpr/ppermute | solution.py:32
  27.1 12.9 %collective-permute-start.21 = (f32[5,8,128]{2,1,0:T(8,128)S(1)}, f32[5,8,128]{2,1,0:T(8,128)S(1)}, u32[]{:S(2)}, u32[]{:S(2)}) collective-permute-start(f32[5,8,128]{2,1,0:T(8,128)S(1)} %get-tuple-element.4128), channel_id=1, source_target_pairs={{0,2},{1,3},{2,4},{3,5},{4,6},{5,7},{6,8},{7,9},{8,10},{9,11},{10,... | collective-permute-start | bytes 61448 | tf_op jit(solution)/shard_map/cond/branch_7_fun/while/body/eval_jaxpr/ppermute | solution.py:45
  30.9 9.2 %copy-start.7 = (bf16[3,5,5,8,8,128]{5,4,3,2,1,0:T(8,128)(2,1)S(1)}, bf16[3,5,5,8,8,128]{5,4,3,2,1,0:T(8,128)(2,1)}, u32[]{:S(2)}) copy-start(bf16[3,5,5,8,8,128]{5,4,3,2,1,0:T(8,128)(2,1)} %get-tuple-element.4620) | copy-start | bytes 3686404 | tf_op jit(solution)/shard_map/cond/branch_7_fun/while
  30.9 9.2 %copy-start.37 = (f32[5,8,8,128]{3,2,1,0:T(8,128)S(1)}, f32[5,8,8,128]{3,2,1,0:T(8,128)}, u32[]{:S(2)}) copy-start(f32[5,8,8,128]{3,2,1,0:T(8,128)} %get-tuple-element.4624) | copy-start | bytes 491524 | tf_op jit(solution)/shard_map/cond/branch_7_fun/while
  32.6 7.1 %collective-permute-start.23 = (f32[5,9,128]{2,1,0:T(8,128)S(1)}, f32[5,9,128]{2,1,0:T(8,128)S(1)}, u32[]{:S(2)}, u32[]{:S(2)}) collective-permute-start(f32[5,9,128]{2,1,0:T(8,128)S(1)} %pad_maximum_fusion.37), channel_id=1, source_target_pairs={{0,30},{1,31},{2,0},{3,1},{4,2},{5,3},{6,4},{7,5},{8,6},{9,7},{10,... | collective-permute-start | bytes 69128 | tf_op jit(solution)/shard_map/cond/branch_7_fun/while/body/eval_jaxpr/ppermute | solution.py:47
  40.1 1.0 %copy-start.22 = (bf16[5,5,8,8,128]{4,3,2,1,0:T(8,128)(2,1)S(1)}, bf16[5,5,8,8,128]{4,3,2,1,0:T(8,128)(2,1)}, u32[]{:S(2)}) copy-start(bf16[5,5,8,8,128]{4,3,2,1,0:T(8,128)(2,1)} %get-tuple-element.4619) | copy-start | bytes 1228804 | tf_op jit(solution)/shard_map/cond/branch_7_fun/while
  42.6 6.0 %collective-permute-start.22 = (f32[5,8,128]{2,1,0:T(8,128)S(1)}, f32[5,8,128]{2,1,0:T(8,128)S(1)}, u32[]{:S(2)}, u32[]{:S(2)}) collective-permute-start(f32[5,8,128]{2,1,0:T(8,128)S(1)} %fusion.832), channel_id=1, source_target_pairs={{1,0},{3,2},{5,4},{7,6},{9,8},{11,10},{13,12},{15,14},{17,16},{19,... | collective-permute-start | bytes 61448 | tf_op jit(solution)/shard_map/cond/branch_7_fun/while/body/eval_jaxpr/ppermute | solution.py:32
  43.6 12.9 %collective-permute-start.21 = (f32[5,8,128]{2,1,0:T(8,128)S(1)}, f32[5,8,128]{2,1,0:T(8,128)S(1)}, u32[]{:S(2)}, u32[]{:S(2)}) collective-permute-start(f32[5,8,128]{2,1,0:T(8,128)S(1)} %get-tuple-element.4128), channel_id=1, source_target_pairs={{0,2},{1,3},{2,4},{3,5},{4,6},{5,7},{6,8},{7,9},{8,10},{9,11},{10,... | collective-permute-start | bytes 61448 | tf_op jit(solution)/shard_map/cond/branch_7_fun/while/body/eval_jaxpr/ppermute | solution.py:45
  46.8 9.8 %copy-start.7 = (bf16[3,5,5,8,8,128]{5,4,3,2,1,0:T(8,128)(2,1)S(1)}, bf16[3,5,5,8,8,128]{5,4,3,2,1,0:T(8,128)(2,1)}, u32[]{:S(2)}) copy-start(bf16[3,5,5,8,8,128]{5,4,3,2,1,0:T(8,128)(2,1)} %get-tuple-element.4620) | copy-start | bytes 3686404 | tf_op jit(solution)/shard_map/cond/branch_7_fun/while
  46.8 9.8 %copy-start.37 = (f32[5,8,8,128]{3,2,1,0:T(8,128)S(1)}, f32[5,8,8,128]{3,2,1,0:T(8,128)}, u32[]{:S(2)}) copy-start(f32[5,8,8,128]{3,2,1,0:T(8,128)} %get-tuple-element.4624) | copy-start | bytes 491524 | tf_op jit(solution)/shard_map/cond/branch_7_fun/while
  48.6 7.6 %collective-permute-start.23 = (f32[5,9,128]{2,1,0:T(8,128)S(1)}, f32[5,9,128]{2,1,0:T(8,128)S(1)}, u32[]{:S(2)}, u32[]{:S(2)}) collective-permute-start(f32[5,9,128]{2,1,0:T(8,128)S(1)} %pad_maximum_fusion.37), channel_id=1, source_target_pairs={{0,30},{1,31},{2,0},{3,1},{4,2},{5,3},{6,4},{7,5},{8,6},{9,7},{10,... | collective-permute-start | bytes 69128 | tf_op jit(solution)/shard_map/cond/branch_7_fun/while/body/eval_jaxpr/ppermute | solution.py:47
  56.6 1.0 %copy-start.22 = (bf16[5,5,8,8,128]{4,3,2,1,0:T(8,128)(2,1)S(1)}, bf16[5,5,8,8,128]{4,3,2,1,0:T(8,128)(2,1)}, u32[]{:S(2)}) copy-start(bf16[5,5,8,8,128]{4,3,2,1,0:T(8,128)(2,1)} %get-tuple-element.4619) | copy-start | bytes 1228804 | tf_op jit(solution)/shard_map/cond/branch_7_fun/while
  59.1 6.0 %collective-permute-start.22 = (f32[5,8,128]{2,1,0:T(8,128)S(1)}, f32[5,8,128]{2,1,0:T(8,128)S(1)}, u32[]{:S(2)}, u32[]{:S(2)}) collective-permute-start(f32[5,8,128]{2,1,0:T(8,128)S(1)} %fusion.832), channel_id=1, source_target_pairs={{1,0},{3,2},{5,4},{7,6},{9,8},{11,10},{13,12},{15,14},{17,16},{19,... | collective-permute-start | bytes 61448 | tf_op jit(solution)/shard_map/cond/branch_7_fun/while/body/eval_jaxpr/ppermute | solution.py:32
  60.1 12.9 %collective-permute-start.21 = (f32[5,8,128]{2,1,0:T(8,128)S(1)}, f32[5,8,128]{2,1,0:T(8,128)S(1)}, u32[]{:S(2)}, u32[]{:S(2)}) collective-permute-start(f32[5,8,128]{2,1,0:T(8,128)S(1)} %get-tuple-element.4128), channel_id=1, source_target_pairs={{0,2},{1,3},{2,4},{3,5},{4,6},{5,7},{6,8},{7,9},{8,10},{9,11},{10,... | collective-permute-start | bytes 61448 | tf_op jit(solution)/shard_map/cond/branch_7_fun/while/body/eval_jaxpr/ppermute | solution.py:45
  63.4 9.8 %copy-start.7 = (bf16[3,5,5,8,8,128]{5,4,3,2,1,0:T(8,128)(2,1)S(1)}, bf16[3,5,5,8,8,128]{5,4,3,2,1,0:T(8,128)(2,1)}, u32[]{:S(2)}) copy-start(bf16[3,5,5,8,8,128]{5,4,3,2,1,0:T(8,128)(2,1)} %get-tuple-element.4620) | copy-start | bytes 3686404 | tf_op jit(solution)/shard_map/cond/branch_7_fun/while
  63.4 9.8 %copy-start.37 = (f32[5,8,8,128]{3,2,1,0:T(8,128)S(1)}, f32[5,8,8,128]{3,2,1,0:T(8,128)}, u32[]{:S(2)}) copy-start(f32[5,8,8,128]{3,2,1,0:T(8,128)} %get-tuple-element.4624) | copy-start | bytes 491524 | tf_op jit(solution)/shard_map/cond/branch_7_fun/while
  65.1 7.7 %collective-permute-start.23 = (f32[5,9,128]{2,1,0:T(8,128)S(1)}, f32[5,9,128]{2,1,0:T(8,128)S(1)}, u32[]{:S(2)}, u32[]{:S(2)}) collective-permute-start(f32[5,9,128]{2,1,0:T(8,128)S(1)} %pad_maximum_fusion.37), channel_id=1, source_target_pairs={{0,30},{1,31},{2,0},{3,1},{4,2},{5,3},{6,4},{7,5},{8,6},{9,7},{10,... | collective-permute-start | bytes 69128 | tf_op jit(solution)/shard_map/cond/branch_7_fun/while/body/eval_jaxpr/ppermute | solution.py:47
  73.1 1.0 %copy-start.22 = (bf16[5,5,8,8,128]{4,3,2,1,0:T(8,128)(2,1)S(1)}, bf16[5,5,8,8,128]{4,3,2,1,0:T(8,128)(2,1)}, u32[]{:S(2)}) copy-start(bf16[5,5,8,8,128]{4,3,2,1,0:T(8,128)(2,1)} %get-tuple-element.4619) | copy-start | bytes 1228804 | tf_op jit(solution)/shard_map/cond/branch_7_fun/while
